TPU v7x, 16 devices: a whole 2x2x2 slice. The times are simulated.
16 devices in a mesh: dp: 2 (over z), sp: 8 (over y, x, core).
Axes of the slice: x: 2, y: 2, z: 2, core: 2. Of those that a mesh axis runs over, the one named last changes fastest.
Arguments:
- x: bfloat16 [64, 512, 128], P('dp', 'sp'), parts along dimension 0
- w_cur: bfloat16 [16, 8, 128, 256], replicated
- w_past: bfloat16 [16, 8, 128, 256], replicated
- w_res: bfloat16 [16, 8, 128, 128], replicated
- w_skip: bfloat16 [16, 8, 128, 128], replicated
Outputs:
- output 1: float32 [64, 8, 64, 128], P('dp', 'sp'), parts along dimension 0
- output 2: float32 [64, 8, 64, 128], P('dp', 'sp'), parts along dimension 0
There are 2 independent parts. A program takes and returns all parts, laid end to end along the dimension named above; an argument that names none is the same for every part.
All inputs are finite; a program needn't handle non-finite values.
Results may differ from a plain program's by a relative error of at most 0.00860394.
Values are sent between devices in bfloat16 or wider.
A program may use at most 1 GiB of HBM per device.

v0:
```python
import functools

import jax
import jax.numpy as jnp
from jax import lax
from jax.experimental import pallas as pl
from jax.experimental.pallas import tpu as pltpu
from jax.sharding import PartitionSpec as P

MESH = pl.DeviceIdType.MESH
ROWS = 128
ZPAD = 128
HPAD = 8
GROUPS = 2
LEAD = 5
VMEM_MIB = 40
SOLO = (128, 3, 6)
BOTH = (256, 2, 4)
F32 = jnp.float32
BF16 = jnp.bfloat16


def kernel(group_n, seqs, seq_len, stacks, cycle_len, x_ref, wc_hbm, wp_hbm, wr_hbm, ws_hbm, h_out, s_out,
           xin, h_buf, u_buf, a_buf, skip, wc, wp, wr, ws, h_st, s_st,
           in_send, in_recv, out_send, out_recv, w_sem, own_sem):
    me = lax.axis_index("sp")
    seq_dev = seq_len // group_n
    part = seqs // GROUPS
    peers = {}
    for flip in range(1, group_n):
        peer, unit = 0, 1
        while unit < group_n:
            bit = lax.rem(me // unit, 2)
            peer = peer + unit * (1 - bit if flip // unit % 2 else bit)
            unit *= 2
        peers[flip] = peer
    order = sorted(peers, reverse=True)
    weights = ((wc_hbm, wc), (wp_hbm, wp), (wr_hbm, wr), (ws_hbm, ws))

    def weight_copy(stack, which):
        src, dst = weights[which]
        return pltpu.make_async_copy(src.at[stack], dst.at[stack], w_sem.at[which, stack])

    barrier = pltpu.get_barrier_semaphore()
    for flip in order:
        pl.semaphore_signal(barrier, inc=1, device_id={"sp": peers[flip]}, device_id_type=MESH)
    own_in = pltpu.make_async_copy(x_ref.at[pl.ds(me * seqs, seqs)], xin.at[:, pl.ds(me * seq_dev, seq_dev)], own_sem.at[0])
    own_in.start()
    for which in range(4):
        weight_copy(0, which).start()
    zeros_z = jnp.zeros((ZPAD, 128), BF16)
    zeros_h = jnp.zeros((HPAD, 128), F32)
    for b in range(seqs):
        for side in range(2):
            u_buf[side, b, 0:ZPAD, :] = zeros_z
            h_buf[side, b, 0:HPAD, :] = zeros_h
        skip[b] = jnp.zeros((seq_len, 128), F32)
    pl.semaphore_wait(barrier, group_n - 1)

    in_copies = [[] for _ in range(GROUPS)]
    for g in range(GROUPS):
        for flip in order:
            peer = peers[flip]
            copy = pltpu.make_async_remote_copy(
                src_ref=x_ref.at[pl.ds(peer * seqs + g * part, part)],
                dst_ref=xin.at[pl.ds(g * part, part), pl.ds(me * seq_dev, seq_dev)],
                send_sem=in_send.at[g, flip - 1], recv_sem=in_recv.at[g, flip - 1], device_id={"sp": peer}, device_id_type=MESH)
            copy.start()
            in_copies[g].append(copy)
    for stack in range(1, stacks):
        for which in range(4):
            weight_copy(stack, which).start()

    own_in.wait()

    def past(side, b, first, rows, dilation):
        if dilation < 16:
            start = HPAD + first - dilation
            return h_buf[side, b, start:start + rows, :].astype(BF16)
        start = ZPAD + first - dilation
        return u_buf[side, b, start:start + rows, :]

    def load_input(g):
        for copy in in_copies[g]:
            copy.wait()
        for b in range(g * part, (g + 1) * part):
            for q in range(seq_len // ROWS):
                piece = xin[b, q * ROWS:(q + 1) * ROWS, :]
                u_buf[0, b, ZPAD + q * ROWS:ZPAD + (q + 1) * ROWS, :] = piece
                h_buf[0, b, HPAD + q * ROWS:HPAD + (q + 1) * ROWS, :] = piece.astype(F32)

    def run(streams, rows, lag1, lag2, paired=True):
        tasks = []
        for k in range(max(len(layers) for _, layers in streams)):
            for g, layers in streams:
                per = max(len(other) for _, other in streams) // len(layers)
                cells = [(b, q) for q in range(seq_len // rows) for b in range(g * part, (g + 1) * part)]
                share = len(cells) // per
                stack, layer = layers[k // per]
                tasks += [(stack, layer, b, q) for b, q in cells[k % per * share:(k % per + 1) * share]]
        zs, rs, gs = {}, {}, []

        def do_z(stack, layer, b, q):
            side = layer % 2
            u = u_buf[side, b, ZPAD + q * rows:ZPAD + (q + 1) * rows, :]
            lhs = jnp.concatenate([u, past(side, b, q * rows, rows, 2 ** layer)], axis=1)
            zs[b, q] = jnp.dot(lhs, jnp.concatenate([wc[stack, layer], wp[stack, layer]], axis=0), preferred_element_type=F32)

        def do_gate(stack, layer, b, q):
            z = zs.pop((b, q))
            a = (jnp.tanh(z[:, :128]) * jax.nn.sigmoid(z[:, 128:])).astype(BF16)
            span = slice(q * rows, (q + 1) * rows)
            w_res = wr[stack, layer]
            zero = jnp.zeros_like(w_res)
            if not paired:
                r = jnp.dot(a, jnp.concatenate([w_res, ws[stack, layer]], axis=1), preferred_element_type=F32)
                rs[b, q] = r[:, :128], r[:, 128:]
            elif layer % 2 == 0:
                a_buf[b, span, :] = a
                gs.append(((b, q), a))
                if len(gs) == 2:
                    (cell0, a0), (cell1, a1) = gs
                    gs.clear()
                    diag = jnp.concatenate([jnp.concatenate([w_res, zero], axis=1), jnp.concatenate([zero, w_res], axis=1)], axis=0)
                    r = jnp.dot(jnp.concatenate([a0, a1], axis=1), diag, preferred_element_type=F32)
                    rs[cell0] = r[:, :128], None
                    rs[cell1] = r[:, 128:], None
            else:
                top = jnp.concatenate([zero, ws[stack, layer - 1]], axis=1)
                rhs = jnp.concatenate([top, jnp.concatenate([w_res, ws[stack, layer]], axis=1)], axis=0)
                r = jnp.dot(jnp.concatenate([a_buf[b, span, :], a], axis=1), rhs, preferred_element_type=F32)
                rs[b, q] = r[:, :128], r[:, 128:]

        def do_update(stack, layer, b, q):
            side = layer % 2
            dh, ds = rs.pop((b, q))
            h_rows = slice(HPAD + q * rows, HPAD + (q + 1) * rows)
            h_new = h_buf[side, b, h_rows, :] + dh
            h_buf[1 - side, b, h_rows, :] = h_new
            u_buf[1 - side, b, ZPAD + q * rows:ZPAD + (q + 1) * rows, :] = h_new.astype(BF16)
            if ds is not None:
                s_rows = slice(q * rows, (q + 1) * rows)
                skip[b, s_rows, :] = skip[b, s_rows, :] + ds

        for k in range(len(tasks) + lag2):
            if k < len(tasks):
                do_z(*tasks[k])
            if 0 <= k - lag1 < len(tasks):
                do_gate(*tasks[k - lag1])
            if 0 <= k - lag2 < len(tasks):
                do_update(*tasks[k - lag2])

    def layers_of(stack):
        return [(stack, layer) for layer in range(cycle_len)]

    def first_use(stack):
        for which in range(4):
            weight_copy(stack, which).wait()

    copies = []

    def send_output(g):
        group_rows = pl.ds(g * part, part)
        pairs = ((h_st, h_out), (s_st, s_out))

        def stage(peer):
            for b in range(g * part, (g + 1) * part):
                h_st[peer, b] = h_buf[0, b, pl.ds(HPAD + peer, seq_dev, stride=group_n), :]
                s_st[peer, b] = skip[b, pl.ds(peer, seq_dev, stride=group_n), :]

        def send(flip):
            for which, (src, dst) in enumerate(pairs):
                copy = pltpu.make_async_remote_copy(
                    src_ref=src.at[peers[flip], group_rows], dst_ref=dst.at[pl.ds(me * seqs + g * part, part)],
                    send_sem=out_send.at[g, which, flip - 1], recv_sem=out_recv.at[g, which, flip - 1],
                    device_id={"sp": peers[flip]}, device_id_type=MESH)
                copy.start()
                copies.append(copy)

        for place, flip in enumerate(order):
            stage(peers[flip])
            if place:
                send(order[place - 1])
        stage(me)
        send(order[-1])
        for which, (src, dst) in enumerate(pairs):
            copy = pltpu.make_async_copy(src.at[me, group_rows], dst.at[pl.ds(me * seqs + g * part, part)], own_sem.at[1 + 2 * g + which])
            copy.start()
            copies.append(copy)

    def only_first(stack, carry):
        first_use(stack)
        run([(0, layers_of(stack))], *SOLO)
        return carry

    def both(stack, carry):
        first_use(stack + LEAD)
        run([(0, layers_of(stack + LEAD)), (1, layers_of(stack))], *BOTH)
        return carry

    def only_second(stack, carry):
        run([(1, layers_of(stack))], *SOLO)
        return carry

    load_input(0)
    lax.fori_loop(0, LEAD, only_first, 0)
    load_input(1)
    lax.fori_loop(0, stacks - LEAD, both, 0)
    send_output(0)
    lax.fori_loop(stacks - LEAD, stacks, only_second, 0)
    send_output(1)
    for copy in copies:
        copy.wait()


def solution(mesh):
    group_n = mesh.shape["sp"]

    def local(x_loc, w_cur, w_past, w_res, w_skip):
        batch, seq_dev, channels = x_loc.shape
        stacks, cycle_len = w_cur.shape[:2]
        seqs, seq_len = batch // group_n, seq_dev * group_n
        any_spec = pl.BlockSpec(memory_space=pl.ANY)
        out = jax.ShapeDtypeStruct((batch, seq_dev, channels), F32)
        args = [pltpu.with_memory_space_constraint(v, pltpu.HBM) for v in (x_loc, w_cur, w_past, w_res, w_skip)]
        h_out, s_out = pl.pallas_call(
            functools.partial(kernel, group_n, seqs, seq_len, stacks, cycle_len),
            out_shape=(out, out),
            in_specs=[any_spec] * 5,
            out_specs=(any_spec, any_spec),
            scratch_shapes=[
                pltpu.VMEM((seqs, seq_len, channels), BF16),
                pltpu.VMEM((2, seqs, HPAD + seq_len, channels), F32),
                pltpu.VMEM((2, seqs, ZPAD + seq_len, channels), BF16),
                pltpu.VMEM((seqs, seq_len, channels), BF16),
                pltpu.VMEM((seqs, seq_len, channels), F32),
                pltpu.VMEM(w_cur.shape, BF16),
                pltpu.VMEM(w_past.shape, BF16),
                pltpu.VMEM(w_res.shape, BF16),
                pltpu.VMEM(w_skip.shape, BF16),
                pltpu.VMEM((group_n, seqs, seq_dev, channels), F32),
                pltpu.VMEM((group_n, seqs, seq_dev, channels), F32),
                pltpu.SemaphoreType.DMA((GROUPS, group_n - 1)),
                pltpu.SemaphoreType.DMA((GROUPS, group_n - 1)),
                pltpu.SemaphoreType.DMA((GROUPS, 2, group_n - 1)),
                pltpu.SemaphoreType.DMA((GROUPS, 2, group_n - 1)),
                pltpu.SemaphoreType.DMA((4, stacks)),
                pltpu.SemaphoreType.DMA((1 + 2 * GROUPS,)),
            ],
            compiler_params=pltpu.CompilerParams(collective_id=0, has_side_effects=True, vmem_limit_bytes=VMEM_MIB * 1024 * 1024),
        )(*args)
        return h_out.reshape(batch, 1, seq_dev, channels), s_out.reshape(batch, 1, seq_dev, channels)

    return jax.shard_map(local, mesh=mesh, in_specs=(P("dp", "sp", None), P(), P(), P(), P()), out_specs=(P("dp", "sp", None, None), P("dp", "sp", None, None)), check_vma=False)
```

profile of v0, /device:TPU:0, one launch (start us, length us, event | category | flops | bytes accessed | tf_op | source)
XLA Modules:
  0.0 98.6 jit_solution(18194190726340306018)
XLA Ops:
  0.6 96.0 %shard_map.68 = (f32[32,64,128]{2,1,0:T(8,128)S(1)}, f32[32,64,128]{2,1,0:T(8,128)S(1)}) custom-call(bf16[32,64,128]{2,1,0:T(8,128)(2,1)} %x_ref.1, bf16[16,8,128,256]{3,2,1,0:T(8,128)(2,1)} %wc_hbm.1, bf16[16,8,128,256]{3,2,1,0:T(8,128)(2,1)} %wp_hbm.1, bf16[16,8,128,128]{3,2,1,0:T(8,128)(2,1)} %wr_hbm.1, bf16[16,8,128,128]{3,2,1,0:T(8,128)(2,1)} %ws_hbm.1), custom_call_target="tpu_custom_call" | custom-call | tf_op jit(solution)/shard_map/pallas_call | solution.py:226
  96.6 1.0 copy.11
  97.6 1.0 copy.12
where the time goes:
time: 98.7 us; the launch traced here: 98.6 us
  Pallas kernels  96 us (97%)
  local copies, waits for them, and re-layouts  1.94 us (2%)
    pallas_call x1, Pallas kernels, local(): pl.pallas_call(functools.partial(kernel, group_n, seqs, seq_len, stacks,...  96 us

commit v1 on v0

--- a/solution.py
+++ b/solution.py
@@ -13,9 +13,11 @@
 HPAD = 8
 GROUPS = 2
 LEAD = 5
+HEAD = 1
 VMEM_MIB = 40
 SOLO = (128, 3, 6)
 BOTH = (256, 2, 4)
+FAST = (256, 2, 5)
 F32 = jnp.float32
 BF16 = jnp.bfloat16
 
@@ -188,14 +190,24 @@
             copy.start()
             copies.append(copy)
 
+    ahead = LEAD - HEAD
+    level = stacks - HEAD - 2 * ahead
+
     def only_first(stack, carry):
         first_use(stack)
         run([(0, layers_of(stack))], *SOLO)
         return carry
 
-    def both(stack, carry):
-        first_use(stack + LEAD)
-        run([(0, layers_of(stack + LEAD)), (1, layers_of(stack))], *BOTH)
+    def two_to_one(k, carry):
+        stack = HEAD + 2 * k
+        first_use(stack)
+        first_use(stack + 1)
+        run([(0, layers_of(stack) + layers_of(stack + 1)), (1, layers_of(k))], *FAST)
+        return carry
+
+    def one_to_one(k, carry):
+        first_use(HEAD + 2 * ahead + k)
+        run([(0, layers_of(HEAD + 2 * ahead + k)), (1, layers_of(ahead + k))], *BOTH)
         return carry
 
     def only_second(stack, carry):
@@ -203,11 +215,12 @@
         return carry
 
     load_input(0)
-    lax.fori_loop(0, LEAD, only_first, 0)
+    lax.fori_loop(0, HEAD, only_first, 0)
     load_input(1)
-    lax.fori_loop(0, stacks - LEAD, both, 0)
+    lax.fori_loop(0, ahead, two_to_one, 0)
+    lax.fori_loop(0, level, one_to_one, 0)
     send_output(0)
-    lax.fori_loop(stacks - LEAD, stacks, only_second, 0)
+    lax.fori_loop(ahead + level, stacks, only_second, 0)
     send_output(1)
     for copy in copies:
         copy.wait()

time: 98.7 us -> 96 us (0.973)
  Pallas kernels: 96 us -> 93.3 us
    pallas_call x1, Pallas kernels: 96 us -> 93.3 us  [local(): pl.pallas_call(functools.partial(kernel, group_n, seqs, seq_len, stacks,...]
where the time goes in v1:
time: 96 us; the launch traced here: 95.9 us
  Pallas kernels  93.3 us (97%)
  local copies, waits for them, and re-layouts  1.94 us (2%)
    pallas_call x1, Pallas kernels, local(): pl.pallas_call(functools.partial(kernel, group_n, seqs, seq_len, stacks,...  93.3 us
    unnamed x2, local copies, waits for them, and re-layouts  1.94 us

profile of v1, /device:TPU:0, one launch (start us, length us, event | category | flops | bytes accessed | tf_op | source)
XLA Modules:
  0.0 95.9 jit_solution(9980738405073984346)
XLA Ops:
  0.6 93.3 %shard_map.68 = (f32[32,64,128]{2,1,0:T(8,128)S(1)}, f32[32,64,128]{2,1,0:T(8,128)S(1)}) custom-call(bf16[32,64,128]{2,1,0:T(8,128)(2,1)} %x_ref.1, bf16[16,8,128,256]{3,2,1,0:T(8,128)(2,1)} %wc_hbm.1, bf16[16,8,128,256]{3,2,1,0:T(8,128)(2,1)} %wp_hbm.1, bf16[16,8,128,128]{3,2,1,0:T(8,128)(2,1)} %wr_hbm.1, bf16[16,8,128,128]{3,2,1,0:T(8,128)(2,1)} %ws_hbm.1), custom_call_target="tpu_custom_call" | custom-call | tf_op jit(solution)/shard_map/pallas_call | solution.py:239
  94.0 1.0 %copy.11 = f32[32,1,64,128]{3,2,1,0:T(8,128)} copy(f32[32,1,64,128]{3,2,1,0:T(8,128)S(1)} %bitcast.7) | data formatting | bytes 2097152
  95.0 1.0 %copy.12 = f32[32,1,64,128]{3,2,1,0:T(8,128)} copy(f32[32,1,64,128]{3,2,1,0:T(8,128)S(1)} %bitcast.6) | data formatting | bytes 2097152
